TPU v7x, 256 devices: a whole 4x4x8 slice. The times are simulated.
256 devices in a mesh: rep: 2 (over y_hi), fsdp: 128 (over z, x, y_lo, core).
Axes of the slice: x: 4, y: 4 (y_hi: 2, y_lo: 2; y = y_hi * 2 + y_lo), z: 8, core: 2. Of those that a mesh axis runs over, the one named last changes fastest.
Arguments:
- tokens: bfloat16 [131072, 4096], P(('rep', 'fsdp')), may hold values from -24 to 24
- value_cot: bfloat16 [131072, 1024], P(('rep', 'fsdp')), may hold values from -6 to 6
- value_weight: bfloat16 [2, 4096, 1024], P('rep', 'fsdp'), may hold values from -0.09375 to 0.09375
- global_params: float32 [16777216], P('fsdp'), may hold values from -6 to 6
- local_params: float32 [2, 16777216], P('rep', 'fsdp'), may hold values from -6 to 6
- momentum: float32 [16777216], P('fsdp'), may hold values from -3 to 3
Outputs:
- token_grad: bfloat16 [131072, 4096], P(('rep', 'fsdp'))
- value_grad: float32 [2, 4096, 1024], P('rep', 'fsdp')
- new_global: float32 [16777216], P('fsdp')
- new_moment: float32 [16777216], P('fsdp')
All inputs are finite; a program needn't handle non-finite values.
Results may differ from a plain program's by a relative error of at most 0.001.
Values may be sent and summed in bfloat16 or wider, within the bound.
No kernel may reach another device: no remote copies, remote signals or barrier semaphores. Data moves between devices by JAX's collectives and lax.ppermute only.
A program may use at most 128 MiB of HBM per device.

v0:
```python
import jax
import jax.numpy as jnp
from jax import lax
from jax.sharding import Mesh
from jax.sharding import PartitionSpec as P

FSDP = ("fsdp_0", "fsdp_1", "fsdp_2", "fsdp_3")
REP_FSDP = ("rep", "fsdp_0", "fsdp_1", "fsdp_2", "fsdp_3")


def split_up(x, dim, length):
    before, after = (x.shape[:dim], x.shape[dim + 1 :])
    return jnp.moveaxis(x.reshape(*before, length, -1, *after), dim, 0)


def summed_rows(x, chips, core, dim):
    sizes = (lax.axis_size(chips), lax.axis_size(core))
    tiles = split_up(x, dim, sizes[0] * sizes[1])
    inside = tiles.shape[1:]
    tiles = tiles.reshape(*sizes, *inside).swapaxes(0, 1).reshape(-1, *inside)
    tiles = lax.psum_scatter(tiles, core, scatter_dimension=0, tiled=True)
    return lax.psum_scatter(tiles, chips, scatter_dimension=0, tiled=True)[0]


def copy_for_each(x, axis):
    length = lax.axis_size(axis)
    return lax.all_to_all(jnp.broadcast_to(x[None], (length, *x.shape)), axis, 0, 0, tiled=True)


def over_copies(x, axis):
    everything = copy_for_each(x, axis)
    return jnp.sum(everything, axis=0)


def grad_term(tokens, columns):
    return lax.dot_general(
        tokens, columns, (((0,), (0,)), ((), ())), preferred_element_type=jnp.float32
    )


def shards(tokens, value_cot, value_weight, global_params, local_params, momentum):
    weight = value_weight[0]
    token_grad = lax.dot_general(
        value_cot,
        lax.all_gather(weight, FSDP, axis=0, tiled=True),
        (((1,), (1,)), ((), ())),
        preferred_element_type=jnp.float32,
    ).astype(jnp.bfloat16)
    groups = lax.axis_size(FSDP)
    factor = 1.0 / jnp.sqrt(jnp.float32(tokens.shape[0] * groups))
    summed = summed_rows(grad_term(tokens, value_cot), ("fsdp_0", "fsdp_1", "fsdp_2"), "fsdp_3", 0)
    value_grad = (summed * factor)[None]
    totals = over_copies(local_params[0], "rep")
    pseudo = global_params - totals / lax.axis_size("rep")
    new_moment = 0.9 * momentum + pseudo
    new_global = global_params - 0.7 * (pseudo + 0.9 * new_moment)
    return (token_grad, value_grad, new_global, new_moment)


def solution(mesh):
    split = Mesh(
        mesh.devices.reshape(mesh.shape["rep"], 8, 4, 2, 2),
        ("rep", "fsdp_0", "fsdp_1", "fsdp_2", "fsdp_3"),
    )
    return jax.shard_map(
        shards,
        mesh=split,
        in_specs=(
            P(REP_FSDP, None),
            P(REP_FSDP, None),
            P("rep", FSDP, None),
            P(FSDP),
            P("rep", FSDP),
            P(FSDP),
        ),
        out_specs=(P(REP_FSDP, None), P("rep", FSDP, None), P(FSDP), P(FSDP)),
        check_vma=False,
    )
```

profile of v0, /device:TPU:16, one launch (start us, length us, event | category | flops | bytes accessed | tf_op | source)
XLA Modules:
  0.0 405.7 jit_solution(8462821204067004481)
XLA Ops:
  8.0 0.0 copy-start
  8.0 0.0 reduce-scatter.3.cloned.1.call-start
  8.1 1.2 copy-done
  9.2 6.5 %fusion.5 = f32[4096,1024]{1,0:T(8,128)S(1)} fusion(bf16[512,4096]{1,0:T(8,128)(2,1)} %param.6, bf16[512,1024]{1,0:T(8,128)(2,1)S(1)} %copy-done), kind=kOutput, calls=%fused_computation.7 | convolution fusion | flops 4294967296 | bytes 22020096 | tf_op jit(solution)/shard_map/dot_general | solution.py:36
  15.7 6.1 %copy.12 = f32[2,64,32,1024]{3,2,1,0:T(8,128)} copy(f32[2,64,32,1024]{3,2,0,1:T(8,128)S(1)} %bitcast.14) | data formatting | bytes 33554432 | tf_op jit(solution)/shard_map/transpose | solution.py:20
  21.8 0.0 reduce-scatter.3.cloned.1.call-update
  21.8 0.0 copy-start.1
  21.8 0.0 copy-start.2
  21.8 0.0 all-gather.3.cloned.1.call-start
  21.9 0.5 all-gather.3.cloned.1.call-update
  22.4 0.0 reduce-scatter.5.cloned.1.call-start
  22.5 32.8 %reduce-scatter.3.cloned.1.call-done = f32[64,32,1024]{2,1,0:T(8,128)} async-done(((f32[128,32,1024]{2,1,0:T(8,128)}), f32[64,32,1024]{2,1,0:T(8,128)}) %reduce-scatter.3.cloned.1.call-update) | async-done | bytes 8388624 | tf_op jit(solution)/shard_map/reduce_scatter | solution.py:21
  55.3 0.0 reduce-scatter.5.cloned.1.call-update
  55.3 0.0 copy-done.1
  55.3 0.5 broadcast_in_dim.2
  55.9 19.6 %all_to_all.6 = f32[2,1,131072]{2,1,0:T(1,128)S(1)} all-to-all(f32[2,1,131072]{2,1,0:T(1,128)S(1)} %broadcast_in_dim.2), channel_id=1, replica_groups=mesh['rep'=2,'fsdp_0'=8,'fsdp_1'=4,'fsdp_2'=2,'fsdp_3'=2] {'rep'}, dimensions={0} | all-to-all | bytes 2097152 | tf_op jit(solution)/shard_map/all_to_all | solution.py:27
  75.4 1.5 reduce_sum.9
  76.9 0.0 copy-done.2
  76.9 2.1 multiply_subtract_fusion
  79.1 173.3 %all-gather.3.cloned.1.call-done = bf16[1,4096,1024]{2,1,0:T(8,128)(2,1)} async-done(((bf16[1,32,1024]{2,1,0:T(8,128)(2,1)}), bf16[1,4096,1024]{2,1,0:T(8,128)(2,1)}) %all-gather.3.cloned.1.call-update) | async-done | bytes 8388624 | tf_op jit(solution)/shard_map/all_gather | solution.py:45
  252.4 9.5 %fusion.2 = bf16[512,4096]{1,0:T(8,128)(2,1)} fusion(bf16[512,1024]{1,0:T(8,128)(2,1)S(1)} %copy-done, bf16[1,4096,1024]{2,1,0:T(8,128)(2,1)} %all-gather.3.cloned.1.call-done), kind=kOutput, calls=%fused_computation.2 | convolution fusion | flops 4297064448 | bytes 13631488 | tf_op jit(solution)/shard_map/dot_general | solution.py:43
  261.9 134.8 %reduce-scatter.5.cloned.1.call-done = f32[1,32,1024]{2,1,0:T(8,128)} async-done(((f32[64,32,1024]{2,1,0:T(8,128)}), f32[1,32,1024]{2,1,0:T(8,128)}) %reduce-scatter.5.cloned.1.call-update) | async-done | bytes 131088 | tf_op jit(solution)/shard_map/reduce_scatter | solution.py:22
  396.7 1.6 broadcast_multiply_fusion
Async XLA Ops:
  8.0 1.2 copy-start
  8.0 47.3 %reduce-scatter.3.cloned.1.call-start = ((), (), s32[]{:S(2)}) async-start(), calls=%async_computation.3 | async-start | bytes 25165824 | tf_op jit(solution)/shard_map/reduce_scatter | solution.py:21
  21.8 33.5 %copy-start.1 = (f32[1,131072]{1,0:T(1,128)S(1)}, f32[1,131072]{1,0:T(1,128)}, u32[]{:S(2)}) copy-start(f32[1,131072]{1,0:T(1,128)} %param.10) | copy-start | bytes 1572868
  21.8 55.1 %copy-start.2 = (f32[131072]{0:T(1024)S(1)}, f32[131072]{0:T(1024)}, u32[]{:S(2)}) copy-start(f32[131072]{0:T(1024)} %param.9) | copy-start | bytes 1572868
  21.8 230.5 %all-gather.3.cloned.1.call-start = ((), (), s32[]{:S(2)}) async-start(), calls=%async_computation.5 | async-start | bytes 8454144 | tf_op jit(solution)/shard_map/all_gather | solution.py:45
  22.4 374.3 %reduce-scatter.5.cloned.1.call-start = ((), (), s32[]{:S(2)}) async-start(), calls=%async_computation.4 | async-start | bytes 8519680 | tf_op jit(solution)/shard_map/reduce_scatter | solution.py:22
Sparse Core Ops, SparseCore 0:
  21.9 33.3 reduce-scatter.2
  57.8 338.8 reduce-scatter.4
Sparse Core Ops, SparseCore 1:
  24.2 228.1 all-gather.2
where the time goes:
time: 406 us
  waiting for transfers between devices  341 us (84%)
  blocking collectives  19.6 us (5%)
  matrix products  16 us (4%)
  between operations  15.5 us (4%)
  local copies, waits for them, and re-layouts  7.79 us (2%)
  other arithmetic  5.2 us (1%)
    all_gather x1, waiting for transfers between devices, shards(): lax.all_gather(weight, FSDP, axis=0, tiled=True)  173 us
    reduce_scatter x1, waiting for transfers between devices, summed_rows(): return lax.psum_scatter(tiles, chips, scatter_dimension=0, tiled=True)[0]  135 us
    reduce_scatter x1, waiting for transfers between devices, summed_rows(): tiles = lax.psum_scatter(tiles, core, scatter_dimension=0, tiled=True)  32.8 us
    all_to_all x1, blocking collectives, copy_for_each(): lax.all_to_all(jnp.broadcast_to(x[None], (length, *x.shape)), axis, 0, 0,...  19.6 us
    dot_general x1, matrix products, shards(): lax.dot_general(value_cot, lax.all_gather(weight, FSDP, axis=0, tiled=Tru...  9.49 us
  transfers between devices with their start and end apart: 3, of which 3 were waited for; matrix products, arithmetic and copies ran while one was open for 3% of the time, Pallas kernels for 0%

commit v1 on v0

--- a/solution.py
+++ b/solution.py
@@ -42,7 +42,9 @@
     weight = value_weight[0]
     token_grad = lax.dot_general(
         value_cot,
-        lax.all_gather(weight, FSDP, axis=0, tiled=True),
+        jnp.concatenate(
+            lax.all_to_all(jnp.stack([weight] * lax.axis_size(FSDP)), FSDP, 0, 0), axis=0
+        ),
         (((1,), (1,)), ((), ())),
         preferred_element_type=jnp.float32,
     ).astype(jnp.bfloat16)

time: 406 us -> 478 us (1.18)
  waiting for transfers between devices: 341 us -> 394 us
  starting transfers between devices: 0.12 us -> 14.5 us
  local copies, waits for them, and re-layouts: 7.79 us -> 15.3 us
    all_to_all x0 -> x1, waiting for transfers between devices: none -> 223 us  [shards(): lax.all_to_all(jnp.stack([weight] * lax.axis_size(FSDP)), FSDP, 0, 0)]
    all_gather x1 -> x0, waiting for transfers between devices: 173 us -> none  [shards(): lax.all_gather(weight, FSDP, axis=0, tiled=True)]
    reduce_scatter x1, waiting for transfers between devices: 135 us -> 171 us  [summed_rows(): return lax.psum_scatter(tiles, chips, scatter_dimension=0, tiled=True)[0]]
    reduce_scatter x1, waiting for transfers between devices: 32.8 us -> 0.02 us  [summed_rows(): tiles = lax.psum_scatter(tiles, core, scatter_dimension=0, tiled=True)]
    all_to_all x0 -> x1, starting transfers between devices: none -> 14.4 us  [shards(): lax.all_to_all(jnp.stack([weight] * lax.axis_size(FSDP)), FSDP, 0, 0)]
    another operation x0 -> x1, local copies, waits for them, and re-layouts: none -> 6.46 us  [shards(): jnp.stack([weight] * lax.axis_size(FSDP))]
  transfers between devices with their start and end apart: 3 -> 3, of which waited for: 3 -> 2; matrix products, arithmetic and copies ran while one was open for 3% -> 4% of each run, Pallas kernels for 0% -> 0%
where the time goes in v1:
time: 478 us; the launch traced here: 475 us
  waiting for transfers between devices  394 us (82%)
  blocking collectives  16.4 us (3%)
  matrix products  16 us (3%)
  local copies, waits for them, and re-layouts  15.3 us (3%)
  starting transfers between devices  14.5 us (3%)
  between operations  14.1 us (3%)
  other arithmetic  5.2 us (1%)
    all_to_all x1, waiting for transfers between devices, shards(): lax.all_to_all(jnp.stack([weight] * lax.axis_size(FSDP)), FSDP, 0, 0)  223 us
    reduce_scatter x1, waiting for transfers between devices, summed_rows(): return lax.psum_scatter(tiles, chips, scatter_dimension=0, tiled=True)[0]  171 us
    all_to_all x1, blocking collectives, copy_for_each(): lax.all_to_all(jnp.broadcast_to(x[None], (length, *x.shape)), axis, 0, 0,...  16.4 us
    all_to_all x1, starting transfers between devices, shards(): lax.all_to_all(jnp.stack([weight] * lax.axis_size(FSDP)), FSDP, 0, 0)  14.4 us
  transfers between devices with their start and end apart: 3, of which 2 were waited for; matrix products, arithmetic and copies ran while one was open for 4% of the time, Pallas kernels for 0%

profile of v1, /device:TPU:16, one launch (start us, length us, event | category | flops | bytes accessed | tf_op | source)
XLA Modules:
  0.0 475.3 jit_solution(15904543256004525923)
XLA Ops:
  7.2 0.0 copy-start
  7.2 0.0 reduce-scatter.3.cloned.1.call-start
  7.2 1.2 copy-done
  8.4 6.5 %fusion = f32[4096,1024]{1,0:T(8,128)S(1)} fusion(bf16[512,4096]{1,0:T(8,128)(2,1)} %param.6, bf16[512,1024]{1,0:T(8,128)(2,1)S(1)} %copy-done), kind=kOutput, calls=%fused_computation.5 | convolution fusion | flops 4294967296 | bytes 22020096 | tf_op jit(solution)/shard_map/dot_general | solution.py:36
  14.9 6.1 %copy.12 = f32[2,64,32,1024]{3,2,1,0:T(8,128)} copy(f32[2,64,32,1024]{3,2,0,1:T(8,128)S(1)} %bitcast.12) | data formatting | bytes 33554432 | tf_op jit(solution)/shard_map/transpose | solution.py:20
  21.0 0.0 copy-start.1
  21.0 0.0 reduce-scatter.3.cloned.1.call-update
  21.0 1.0 copy-done.1
  22.0 0.5 broadcast_in_dim.2
  22.5 16.4 %all_to_all.11 = f32[2,1,131072]{2,1,0:T(1,128)S(1)} all-to-all(f32[2,1,131072]{2,1,0:T(1,128)S(1)} %broadcast_in_dim.2), channel_id=1, replica_groups=mesh['rep'=2,'fsdp_0'=8,'fsdp_1'=4,'fsdp_2'=2,'fsdp_3'=2] {'rep'}, dimensions={0} | all-to-all | bytes 2097152 | tf_op jit(solution)/shard_map/all_to_all | solution.py:27
  39.0 0.0 copy-done.3
  39.0 6.5 %stack.3 = bf16[128,32,1024]{2,1,0:T(8,128)(2,1)} broadcast(bf16[32,1024]{1,0:T(8,128)(2,1)S(1)} %bitcast.14), dimensions={1,2} | broadcast | bytes 8454144 | tf_op jit(solution)/shard_map/stack | solution.py:46
  45.4 14.4 %all-to-all-start = ((bf16[128,32,1024]{2,1,0:T(8,128)(2,1)}), bf16[128,32,1024]{2,1,0:T(8,128)(2,1)}, u32[]{:S(2)}, u32[]{:S(2)}) async-start(bf16[128,32,1024]{2,1,0:T(8,128)(2,1)} %stack.3), calls=%async_computation | async-start | bytes 16777216 | tf_op jit(solution)/shard_map/all_to_all | solution.py:46
  59.9 0.0 copy-start.2
  59.9 0.0 reduce-scatter.5.cloned.1.call-start
  59.9 0.0 reduce-scatter.3.cloned.1.call-done
  59.9 0.7 reduce-scatter.5.cloned.1.call-update
  60.6 1.5 reduce_sum.9
  62.1 0.0 copy-done.2
  62.1 2.1 multiply_subtract_fusion
  64.3 222.6 %all-to-all-done = bf16[128,32,1024]{2,1,0:T(8,128)(2,1)} async-done(((bf16[128,32,1024]{2,1,0:T(8,128)(2,1)}), bf16[128,32,1024]{2,1,0:T(8,128)(2,1)}, u32[]{:S(2)}, u32[]{:S(2)}) %all-to-all-start) | async-done | bytes 8388640 | tf_op jit(solution)/shard_map/all_to_all | solution.py:46
  286.9 9.5 %convolution_convert_fusion = bf16[512,4096]{1,0:T(8,128)(2,1)} fusion(bf16[512,1024]{1,0:T(8,128)(2,1)S(1)} %copy-done, bf16[4096,1024]{1,0:T(8,128)(2,1)} %bitcast.1), kind=kOutput, calls=%fused_computation | convolution fusion | flops 4297064448 | bytes 13631488 | tf_op jit(solution)/shard_map/dot_general | solution.py:43
  296.3 170.5 %reduce-scatter.5.cloned.1.call-done = f32[1,32,1024]{2,1,0:T(8,128)} async-done(((f32[64,32,1024]{2,1,0:T(8,128)}), f32[1,32,1024]{2,1,0:T(8,128)}) %reduce-scatter.5.cloned.1.call-update) | async-done | bytes 131088 | tf_op jit(solution)/shard_map/reduce_scatter | solution.py:22
  466.9 1.6 broadcast_multiply_fusion
  (1 shorter events, 0.0 us)
Async XLA Ops:
  7.2 1.2 copy-start
  7.2 52.8 %reduce-scatter.3.cloned.1.call-start = ((), (), s32[]{:S(2)}) async-start(), calls=%async_computation.4 | async-start | bytes 25165824 | tf_op jit(solution)/shard_map/reduce_scatter | solution.py:21
  21.0 1.0 copy-start.1
  21.0 18.0 %copy-start.3 = (bf16[1,32,1024]{2,1,0:T(8,128)(2,1)S(1)}, bf16[1,32,1024]{2,1,0:T(8,128)(2,1)}, u32[]{:S(2)}) copy-start(bf16[1,32,1024]{2,1,0:T(8,128)(2,1)} %param.8) | copy-start | bytes 196612
  45.4 241.4 %all-to-all-start = ((bf16[128,32,1024]{2,1,0:T(8,128)(2,1)}), bf16[128,32,1024]{2,1,0:T(8,128)(2,1)}, u32[]{:S(2)}, u32[]{:S(2)}) async-start(bf16[128,32,1024]{2,1,0:T(8,128)(2,1)} %stack.3), calls=%async_computation | async-start | bytes 16777216 | tf_op jit(solution)/shard_map/all_to_all | solution.py:46
  59.9 2.3 copy-start.2
  59.9 407.0 %reduce-scatter.5.cloned.1.call-start = ((), (), s32[]{:S(2)}) async-start(), calls=%async_computation.5 | async-start | bytes 8519680 | tf_op jit(solution)/shard_map/reduce_scatter | solution.py:22
Sparse Core Ops, SparseCore 0:
  21.1 33.3 reduce-scatter.2
  63.2 403.6 reduce-scatter.4
